TPU v7x, 32 devices: a whole 2x2x4 slice. The times are simulated.
32 devices in a mesh: prow: 4 (over x, core), pcol: 8 (over z, y).
Axes of the slice: x: 2, y: 2, z: 4, core: 2. Of those that a mesh axis runs over, the one named last changes fastest.
Arguments:
- panels: bfloat16 [2, 48, 2048, 256], P(None, 'pcol', 'prow'), may hold values from -0.59765625 to 0.59765625
- inverses: bfloat16 [2, 48, 256, 256], P(None, 'pcol', 'prow'), may hold values from -0.25 to 0.25
- dest: int32 [48, 8, 8], P('pcol', 'prow'), may hold values from 0 to 7, as said below
- target: int32 [48, 8, 8], P('pcol', 'prow'), may hold values from 0 to 1
- ancestors: float32 [2, 2048, 2048], P(None, 'prow', 'pcol'), may hold values from -6 to 6
Outputs:
- factor: bfloat16 [2, 48, 2048, 256], P(None, 'pcol', 'prow')
- schur: float32 [2, 2048, 2048], P(None, 'prow', 'pcol')
Inputs may be any that keep to these rules, and one draw needn't show every extreme that they name: `dest`: among the 96 update blocks of one device (its leaves, its block rows), at most 24 name any one process column; on every process row one process column is named by exactly 24 blocks of every device of that row.
All inputs are finite; a program needn't handle non-finite values.
Results may differ from a plain program's by a relative error of at most 0.0045.
Values may be sent and summed in bfloat16 or wider, within the bound.
No kernel may reach another device: no remote copies, remote signals or barrier semaphores. Data moves between devices by JAX's collectives and lax.ppermute only.
A program may use at most 128 MiB of HBM per device.

v0:
```python
import jax
import jax.numpy as jnp
from jax import lax
from jax.sharding import PartitionSpec as P


def complex_product(left_real, left_imag, right_real, right_imag, pattern):

    def single(first_operand, second):
        return jnp.einsum(pattern, first_operand, second, preferred_element_type=jnp.float32)

    real_part = single(left_real, right_real) - single(left_imag, right_imag)
    imag_part = single(left_real, right_imag) + single(left_imag, right_real)
    return jnp.stack([real_part, imag_part]).astype(jnp.bfloat16)


def local(panels, inverses, dest, target, ancestors):
    inverse_full = lax.all_gather(inverses, "prow", axis=2, tiled=True)
    lower_panel = complex_product(
        panels[0], panels[1], inverse_full[0], inverse_full[1], "lrk,lkc->lrc"
    )
    segment = lax.all_gather(panels, "prow", axis=2, tiled=True)
    update = complex_product(lower_panel[0], lower_panel[1], segment[0], segment[1], "lrk,lck->lrc")
    block_width = panels.shape[3]
    leaf_count = panels.shape[1]
    local_rows = panels.shape[2] // block_width
    front_blocks = update.shape[3] // block_width
    blocks = update.reshape(2, leaf_count, local_rows, block_width, front_blocks, block_width)
    blocks = blocks.transpose(1, 2, 4, 0, 3, 5).reshape(-1, 2, block_width, block_width)
    block_count = blocks.shape[0]
    column_count = lax.axis_size("pcol")
    owned_blocks = ancestors.shape[1] // block_width
    dest_flat = dest.reshape(-1)
    target_flat = target.reshape(-1)
    slot_keys = dest_flat * owned_blocks + target_flat
    select = (
        jnp.arange(column_count * owned_blocks, dtype=jnp.int32)[:, None] == slot_keys[None, :]
    ).astype(jnp.bfloat16)
    merged = jnp.dot(select, blocks.reshape(block_count, -1), preferred_element_type=jnp.float32)
    arrived = lax.all_to_all(
        merged.astype(jnp.bfloat16), "pcol", split_axis=0, concat_axis=0, tiled=True
    ).astype(merged.dtype)
    summed = jnp.sum(arrived.reshape(column_count, owned_blocks, -1), axis=0)
    summed = summed.reshape(owned_blocks, 2, block_width, block_width).transpose(1, 0, 2, 3)
    summed = summed.reshape(2, owned_blocks * block_width, block_width)
    return (lower_panel, ancestors - summed)


def solution(mesh):
    return jax.shard_map(
        local,
        mesh=mesh,
        in_specs=(
            P(None, "pcol", "prow", None),
            P(None, "pcol", "prow", None),
            P("pcol", "prow", None),
            P("pcol", "prow", None),
            P(None, "prow", "pcol"),
        ),
        out_specs=(P(None, "pcol", "prow", None), P(None, "prow", "pcol")),
        check_vma=False,
    )
```

profile of v0, /device:TPU:0, one launch (start us, length us, event | category | flops | bytes accessed | tf_op | source)
XLA Modules:
  0.0 374.9 jit_solution(875081187153657765)
XLA Ops:
  7.2 0.0 all-gather.3.cloned.1.call-start
  7.2 0.7 all-gather.3.cloned.1.call-update
  7.9 0.0 all-gather.5.cloned.1.call-start
  8.0 0.7 all-gather.5.cloned.1.call-update
  8.7 0.1 add.18
  8.8 23.1 %all-gather.3.cloned.1.call-done = bf16[2,6,256,256]{3,2,1,0:T(8,128)(2,1)} async-done(((bf16[2,6,64,256]{3,2,1,0:T(8,128)(2,1)}), bf16[2,6,256,256]{3,2,1,0:T(8,128)(2,1)}) %all-gather.3.cloned.1.call-update) | async-done | bytes 1572880 | tf_op jit(solution)/shard_map/all_gather | solution.py:18
  32.0 1.8 fusion.6
  33.8 0.6 fusion.4
  34.4 1.3 copy-done.1
  35.7 0.6 subtract_convert_fusion.1
  36.3 0.6 add_convert_fusion.1
  36.8 78.8 %all-gather.5.cloned.1.call-done = bf16[2,6,2048,256]{3,2,1,0:T(8,128)(2,1)} async-done(((bf16[2,6,512,256]{3,2,1,0:T(8,128)(2,1)}), bf16[2,6,2048,256]{3,2,1,0:T(8,128)(2,1)}) %all-gather.5.cloned.1.call-update) | async-done | bytes 12582928 | tf_op jit(solution)/shard_map/all_gather | solution.py:22
  115.6 12.9 %fusion.1 = f32[6,512,2048]{2,1,0:T(8,128)} fusion(bf16[6,512,256]{2,1,0:T(8,128)(2,1)S(1)} %subtract_convert_fusion.1, bf16[2,6,2048,256]{3,2,1,0:T(8,128)(2,1)} %all-gather.5.cloned.1.call-done), kind=kOutput, calls=%fused_computation.8 | convolution fusion | flops 3221225472 | bytes 33030144 | tf_op jit(solution)/shard_map/lrk,lck->lrc/dot_general | solution.py:10
  128.5 18.0 %add_convert_fusion = bf16[6,512,2048]{2,1,0:T(8,128)(2,1)} fusion(f32[6,512,2048]{2,1,0:T(8,128)} %fusion.1, bf16[6,512,256]{2,1,0:T(8,128)(2,1)S(1)} %add_convert_fusion.1, bf16[2,6,2048,256]{3,2,1,0:T(8,128)(2,1)} %all-gather.5.cloned.1.call-done), kind=kOutput, calls=%fused_computation.2 | convolution fusion | flops 3233808384 | bytes 45613056 | tf_op jit(solution)/shard_map/lrk,lck->lrc/dot_general | solution.py:10
  146.5 8.3 %copy.13 = bf16[384,8,8,256]{3,2,1,0:T(8,128)(2,1)S(1)} copy(bf16[384,8,8,256]{3,1,2,0:T(8,128)(2,1)} %bitcast.53) | data formatting | bytes 25165824
  154.8 6.0 %copy.10 = bf16[1,6,2,256,8,256]{5,3,0,4,2,1:T(8,128)(2,1)} copy(bf16[1,6,2,256,8,256]{5,4,3,2,1,0:T(8,128)(2,1)S(1)} %bitcast.54) | data formatting | bytes 25165824 | tf_op jit(solution)/shard_map/stack | solution.py:14
  160.8 12.9 %fusion = f32[6,512,2048]{2,1,0:T(8,128)} fusion(bf16[6,512,256]{2,1,0:T(8,128)(2,1)S(1)} %subtract_convert_fusion.1, bf16[2,6,2048,256]{3,2,1,0:T(8,128)(2,1)} %all-gather.5.cloned.1.call-done), kind=kOutput, calls=%fused_computation.7 | convolution fusion | flops 3221225472 | bytes 33030144 | tf_op jit(solution)/shard_map/lrk,lck->lrc/dot_general | solution.py:10
  173.7 18.1 %subtract_convert_fusion = bf16[6,512,2048]{2,1,0:T(8,128)(2,1)} fusion(f32[6,512,2048]{2,1,0:T(8,128)} %fusion, bf16[6,512,256]{2,1,0:T(8,128)(2,1)S(1)} %add_convert_fusion.1, bf16[2,6,2048,256]{3,2,1,0:T(8,128)(2,1)} %all-gather.5.cloned.1.call-done), kind=kOutput, calls=%fused_computation.3 | convolution fusion | flops 3233808384 | bytes 45613056 | tf_op jit(solution)/shard_map/lrk,lck->lrc/dot_general | solution.py:10
  191.7 9.6 %copy.12 = bf16[384,8,8,256]{3,2,1,0:T(8,128)(2,1)S(1)} copy(bf16[384,8,8,256]{3,1,2,0:T(8,128)(2,1)} %bitcast.52) | data formatting | bytes 25165824
  201.4 6.2 %copy.9 = bf16[1,6,2,256,8,256]{5,3,0,4,2,1:T(8,128)(2,1)S(1)} copy(bf16[1,6,2,256,8,256]{5,4,3,2,1,0:T(8,128)(2,1)S(1)} %bitcast.55) | data formatting | bytes 25165824 | tf_op jit(solution)/shard_map/stack | solution.py:14
  207.6 10.0 %maximum_bitcast_fusion = bf16[6,2,8,2,256,256]{5,4,3,2,1,0:T(8,128)(2,1)} fusion(bf16[1,6,2,256,8,256]{5,3,0,4,2,1:T(8,128)(2,1)S(1)} %bitcast.57, bf16[1,6,2,256,8,256]{5,3,0,4,2,1:T(8,128)(2,1)S(1)} %copy.9), kind=kLoop, calls=%fused_computation.1 | loop fusion | flops 12582912 | bytes 50331648 | tf_op jit(solution)/shard_map/transpose | solution.py:29
  217.6 25.1 %reshape_reshape.3 = bf16[96,131072]{1,0:T(8,128)(2,1)} reshape(bf16[6,2,8,2,256,256]{5,4,3,2,1,0:T(8,128)(2,1)} %maximum_bitcast_fusion) | data formatting | bytes 50331648 | tf_op jit(solution)/shard_map/reshape;reshape | solution.py:39
  242.7 12.0 %convolution_convert_fusion = bf16[16,131072]{1,0:T(8,128)(2,1)} fusion(bf16[96,131072]{1,0:T(8,128)(2,1)} %reshape_reshape.3, s32[96]{0:T(128)S(1)} %add.18), kind=kOutput, calls=%fused_computation | convolution fusion | flops 404751872 | bytes 29360512 | tf_op jit(solution)/shard_map/dot_general | solution.py:39
  254.7 5.5 %all_to_all.6 = bf16[8,2,131072]{2,1,0:T(2,128)(2,1)} reshape(bf16[16,131072]{1,0:T(8,128)(2,1)} %convolution_convert_fusion) | data formatting | bytes 8388608 | tf_op jit(solution)/shard_map/all_to_all | solution.py:40
  260.2 5.5 %all-to-all-start = ((bf16[8,2,131072]{2,1,0:T(2,128)(2,1)}), bf16[8,2,131072]{2,1,0:T(2,128)(2,1)}, u32[]{:S(2)}, u32[]{:S(2)}) async-start(bf16[8,2,131072]{2,1,0:T(2,128)(2,1)} %all_to_all.6), calls=%async_computation | async-start | bytes 8388608 | tf_op jit(solution)/shard_map/all_to_all | solution.py:40
  265.7 1.9 pad_maximum_fusion
  267.7 91.8 %all-to-all-done = bf16[8,2,131072]{2,1,0:T(2,128)(2,1)} async-done(((bf16[8,2,131072]{2,1,0:T(2,128)(2,1)}), bf16[8,2,131072]{2,1,0:T(2,128)(2,1)}, u32[]{:S(2)}, u32[]{:S(2)}) %all-to-all-start) | async-done | bytes 4194336 | tf_op jit(solution)/shard_map/all_to_all | solution.py:40
  359.4 6.3 %convert_reduce_fusion = f32[2,131072]{1,0:T(2,128)S(1)} fusion(bf16[8,2,131072]{2,1,0:T(2,128)(2,1)} %all-to-all-done), kind=kLoop, calls=%fused_computation.4 | loop fusion | flops 3932160 | bytes 5242880 | tf_op jit(solution)/shard_map/reduce_sum | solution.py:43
  365.8 0.1 copy.14
  365.8 0.1 copy.11
  365.9 1.1 copy-done.3
  367.0 1.1 bitcast_subtract_fusion
  (18 shorter events, 0.0 us)
Async XLA Ops:
  7.2 24.8 %copy-start = (bf16[2,6,512,256]{3,2,1,0:T(8,128)(2,1)S(1)}, bf16[2,6,512,256]{3,2,1,0:T(8,128)(2,1)}, u32[]{:S(2)}) copy-start(bf16[2,6,512,256]{3,2,1,0:T(8,128)(2,1)} %param.5) | copy-start | bytes 9437188
  7.2 1.5 copy-start.5
  7.2 1.5 copy-start.4
  7.2 24.8 %all-gather.3.cloned.1.call-start = ((), (), s32[]{:S(2)}) async-start(), calls=%async_computation.1 | async-start | bytes 1966080 | tf_op jit(solution)/shard_map/all_gather | solution.py:18
  7.9 107.7 %all-gather.5.cloned.1.call-start = ((), (), s32[]{:S(2)}) async-start(), calls=%async_computation.2 | async-start | bytes 15728640 | tf_op jit(solution)/shard_map/all_gather | solution.py:22
  32.0 1.8 copy-start.2
  33.8 1.9 copy-start.1
  191.7 15.8 %slice-start = ((s8[12582912]{0:T(1024)(128)(4,1)}), s8[4194304]{0:T(1024)(128)(4,1)S(1)}, s32[]{:S(2)}) async-start(s8[12582912]{0:T(1024)(128)(4,1)} %bitcast.56), calls=%async_computation.3 | async-start | bytes 8388608
  191.7 15.8 %slice-start.1 = ((s8[12582912]{0:T(1024)(128)(4,1)}), s8[4194304]{0:T(1024)(128)(4,1)S(1)}, s32[]{:S(2)}) async-start(s8[12582912]{0:T(1024)(128)(4,1)} %bitcast.56), calls=%async_computation.4 | async-start | bytes 8388608
  201.4 6.2 %slice-start.2 = ((s8[12582912]{0:T(1024)(128)(4,1)}), s8[4194304]{0:T(1024)(128)(4,1)S(1)}, s32[]{:S(2)}) async-start(s8[12582912]{0:T(1024)(128)(4,1)} %bitcast.56), calls=%async_computation.5 | async-start | bytes 8388608
  260.2 99.2 %all-to-all-start = ((bf16[8,2,131072]{2,1,0:T(2,128)(2,1)}), bf16[8,2,131072]{2,1,0:T(2,128)(2,1)}, u32[]{:S(2)}, u32[]{:S(2)}) async-start(bf16[8,2,131072]{2,1,0:T(2,128)(2,1)} %all_to_all.6), calls=%async_computation | async-start | bytes 8388608 | tf_op jit(solution)/shard_map/all_to_all | solution.py:40
  365.7 1.2 copy-start.3
Sparse Core Ops, SparseCore 0:
  9.6 22.3 all-gather.2
  33.5 82.0 all-gather.4
where the time goes:
time: 376 us; the launch traced here: 375 us
  waiting for transfers between devices  195 us (52%)
  matrix products  77.3 us (21%)
  local copies, waits for them, and re-layouts  63.4 us (17%)
  other arithmetic  19.3 us (5%)
  between operations  14.2 us (4%)
  starting transfers between devices  5.59 us (1%)
    all_to_all x1, waiting for transfers between devices, local(): lax.all_to_all(merged.astype(jnp.bfloat16), 'pcol', split_axis=0, concat_...  91.8 us
    all_gather x1, waiting for transfers between devices, local(): segment = lax.all_gather(panels, 'prow', axis=2, tiled=True)  78.8 us
    dot_general x8, matrix products, single(): jnp.einsum(pattern, first_operand, second, preferred_element_type=jnp.flo...  65.3 us
    another operation x1, local copies, waits for them, and re-layouts, local(): blocks.reshape(block_count, -1)  25.1 us
    all_gather x1, waiting for transfers between devices, local(): inverse_full = lax.all_gather(inverses, 'prow', axis=2, tiled=True)  23.1 us
    unnamed x21, local copies, waits for them, and re-layouts  20.4 us
    another operation x2, local copies, waits for them, and re-layouts, complex_product(): return jnp.stack([real_part, imag_part]).astype(jnp.bfloat16)  12.2 us
    dot_general x1, matrix products, local(): jnp.dot(select, blocks.reshape(block_count, -1), preferred_element_type=j...  12 us
  transfers between devices with their start and end apart: 3, of which 3 were waited for; matrix products, arithmetic and copies ran while one was open for 1% of the time, Pallas kernels for 0%

commit v1 on v0

--- a/solution.py
+++ b/solution.py
@@ -19,7 +19,15 @@
     lower_panel = complex_product(
         panels[0], panels[1], inverse_full[0], inverse_full[1], "lrk,lkc->lrc"
     )
-    segment = lax.all_gather(panels, "prow", axis=2, tiled=True)
+    ways, here = (lax.axis_size("prow"), lax.axis_index("prow"))
+    grown, reach = (panels, 1)
+    while reach < ways:
+        theirs = lax.ppermute(grown, "prow", [(d, d ^ reach) for d in range(ways)])
+        mine_first = jnp.concatenate([grown, theirs], axis=2)
+        theirs_first = jnp.concatenate([theirs, grown], axis=2)
+        grown = jnp.where(here & reach == 0, mine_first, theirs_first)
+        reach = 2 * reach
+    segment = grown
     update = complex_product(lower_panel[0], lower_panel[1], segment[0], segment[1], "lrk,lck->lrc")
     block_width = panels.shape[3]
     leaf_count = panels.shape[1]

time: 376 us -> 443 us (1.18)
  waiting for transfers between devices: 195 us -> 236 us
  other arithmetic: 19.3 us -> 43.1 us
    ppermute x0 -> x2, waiting for transfers between devices: none -> 117 us  [local(): theirs = lax.ppermute(grown, 'prow', [(d, d ^ reach) for d in range(ways)])]
    all_gather x1 -> x0, waiting for transfers between devices: 78.8 us -> none  [local(): segment = lax.all_gather(panels, 'prow', axis=2, tiled=True)]
    select_n x0 -> x2, other arithmetic: none -> 23.8 us  [local(): grown = jnp.where(here & reach == 0, mine_first, theirs_first)]
    all_gather x1, waiting for transfers between devices: 23.1 us -> 28.5 us  [local(): inverse_full = lax.all_gather(inverses, 'prow', axis=2, tiled=True)]
  transfers between devices with their start and end apart: 3 -> 4, of which waited for: 3 -> 4; matrix products, arithmetic and copies ran while one was open for 1% -> 2% of each run, Pallas kernels for 0% -> 0%
where the time goes in v1:
time: 443 us
  waiting for transfers between devices  236 us (53%)
  matrix products  78.5 us (18%)
  local copies, waits for them, and re-layouts  61.2 us (14%)
  other arithmetic  43.1 us (10%)
  between operations  14.2 us (3%)
  starting transfers between devices  9.53 us (2%)
    ppermute x2, waiting for transfers between devices, local(): theirs = lax.ppermute(grown, 'prow', [(d, d ^ reach) for d in range(ways)])  117 us
    all_to_all x1, waiting for transfers between devices, local(): lax.all_to_all(merged.astype(jnp.bfloat16), 'pcol', split_axis=0, concat_...  90.8 us
    dot_general x8, matrix products, single(): jnp.einsum(pattern, first_operand, second, preferred_element_type=jnp.flo...  66.5 us
    all_gather x1, waiting for transfers between devices, local(): inverse_full = lax.all_gather(inverses, 'prow', axis=2, tiled=True)  28.5 us
    another operation x1, local copies, waits for them, and re-layouts, local(): blocks.reshape(block_count, -1)  25.1 us
    select_n x2, other arithmetic, local(): grown = jnp.where(here & reach == 0, mine_first, theirs_first)  23.8 us
    unnamed x21, local copies, waits for them, and re-layouts  18.1 us
    another operation x2, local copies, waits for them, and re-layouts, complex_product(): return jnp.stack([real_part, imag_part]).astype(jnp.bfloat16)  12.3 us
  transfers between devices with their start and end apart: 4, of which 4 were waited for; matrix products, arithmetic and copies ran while one was open for 2% of the time, Pallas kernels for 0%

profile of v1, /device:TPU:0, one launch (start us, length us, event | category | flops | bytes accessed | tf_op | source)
XLA Modules:
  0.0 442.6 jit_solution(4905330703197903651)
XLA Ops:
  7.2 0.0 all-gather.2.cloned.1.call-start
  7.2 0.6 collective-permute-start
  7.8 5.6 %collective-permute-done = bf16[2,6,512,256]{3,2,1,0:T(8,128)(2,1)} collective-permute-done((bf16[2,6,512,256]{3,2,1,0:T(8,128)(2,1)}, bf16[2,6,512,256]{3,2,1,0:T(8,128)(2,1)}, u32[]{:S(2)}, u32[]{:S(2)}) %collective-permute-start) | collective-permute-done | bytes 3145760 | tf_op jit(solution)/shard_map/ppermute | solution.py:25
  13.4 8.6 %maximum_select_fusion.1 = bf16[2,6,1024,256]{3,2,1,0:T(8,128)(2,1)} fusion(bf16[2,6,512,256]{3,2,1,0:T(8,128)(2,1)} %collective-permute-done, bf16[2,6,512,256]{3,2,1,0:T(8,128)(2,1)} %param.5, pred[]{:T(512)S(6)} %eq.23), kind=kLoop, calls=%fused_computation.8 | loop fusion | flops 28311552 | bytes 12582913 | tf_op jit(solution)/shard_map/jit(_where)/select_n | solution.py:28
  22.0 2.8 collective-permute-start.1
  24.9 0.1 add.18
  25.0 28.5 %all-gather.2.cloned.1.call-done = bf16[2,6,256,256]{3,2,1,0:T(8,128)(2,1)} async-done(((bf16[2,6,64,256]{3,2,1,0:T(8,128)(2,1)}), bf16[2,6,256,256]{3,2,1,0:T(8,128)(2,1)}) %all-gather.2.cloned.1.call-update) | async-done | bytes 1572880 | tf_op jit(solution)/shard_map/all_gather | solution.py:18
  53.5 1.9 fusion.4
  55.3 1.7 fusion.6
  57.1 0.6 add_convert_fusion.1
  57.7 0.6 subtract_convert_fusion.1
  58.2 111.1 %collective-permute-done.1 = bf16[2,6,1024,256]{3,2,1,0:T(8,128)(2,1)} collective-permute-done((bf16[2,6,1024,256]{3,2,1,0:T(8,128)(2,1)}, bf16[2,6,1024,256]{3,2,1,0:T(8,128)(2,1)}, u32[]{:S(2)}, u32[]{:S(2)}) %collective-permute-start.1) | collective-permute-done | bytes 6291488 | tf_op jit(solution)/shard_map/ppermute | solution.py:25
  169.4 15.2 %maximum_select_fusion = bf16[2,6,2048,256]{3,2,1,0:T(8,128)(2,1)} fusion(bf16[2,6,1024,256]{3,2,1,0:T(8,128)(2,1)} %collective-permute-done.1, bf16[2,6,1024,256]{3,2,1,0:T(8,128)(2,1)} %maximum_select_fusion.1, pred[]{:T(512)S(6)} %eq.22), kind=kLoop, calls=%fused_computation.4 | loop fusion | flops 56623104 | bytes 25165824 | tf_op jit(solution)/shard_map/jit(_where)/select_n | solution.py:28
  184.6 12.8 %fusion.1 = f32[6,512,2048]{2,1,0:T(8,128)} fusion(bf16[6,512,256]{2,1,0:T(8,128)(2,1)S(1)} %add_convert_fusion.1, bf16[2,6,2048,256]{3,2,1,0:T(8,128)(2,1)} %maximum_select_fusion), kind=kOutput, calls=%fused_computation.10 | convolution fusion | flops 3221225472 | bytes 33030144 | tf_op jit(solution)/shard_map/lrk,lck->lrc/dot_general | solution.py:10
  197.5 12.9 %fusion = f32[6,512,2048]{2,1,0:T(8,128)} fusion(bf16[6,512,256]{2,1,0:T(8,128)(2,1)S(1)} %add_convert_fusion.1, bf16[2,6,2048,256]{3,2,1,0:T(8,128)(2,1)} %maximum_select_fusion), kind=kOutput, calls=%fused_computation.9 | convolution fusion | flops 3221225472 | bytes 33030144 | tf_op jit(solution)/shard_map/lrk,lck->lrc/dot_general | solution.py:10
  210.3 18.1 %subtract_convert_fusion = bf16[6,512,2048]{2,1,0:T(8,128)(2,1)} fusion(f32[6,512,2048]{2,1,0:T(8,128)} %fusion.1, bf16[6,512,256]{2,1,0:T(8,128)(2,1)S(1)} %subtract_convert_fusion.1, bf16[2,6,2048,256]{3,2,1,0:T(8,128)(2,1)} %maximum_select_fusion), kind=kOutput, calls=%fused_computation.3 | convolution fusion | flops 3233808384 | bytes 45613056 | tf_op jit(solution)/shard_map/lrk,lck->lrc/dot_general | solution.py:10
  228.4 8.3 %copy.12 = bf16[384,8,8,256]{3,2,1,0:T(8,128)(2,1)S(1)} copy(bf16[384,8,8,256]{3,1,2,0:T(8,128)(2,1)} %bitcast.53) | data formatting | bytes 25165824
  236.7 6.1 %copy.9 = bf16[1,6,2,256,8,256]{5,3,0,4,2,1:T(8,128)(2,1)} copy(bf16[1,6,2,256,8,256]{5,4,3,2,1,0:T(8,128)(2,1)S(1)} %bitcast.54) | data formatting | bytes 25165824 | tf_op jit(solution)/shard_map/stack | solution.py:14
  242.8 18.0 %add_convert_fusion = bf16[6,512,2048]{2,1,0:T(8,128)(2,1)} fusion(f32[6,512,2048]{2,1,0:T(8,128)} %fusion, bf16[6,512,256]{2,1,0:T(8,128)(2,1)S(1)} %subtract_convert_fusion.1, bf16[2,6,2048,256]{3,2,1,0:T(8,128)(2,1)} %maximum_select_fusion), kind=kOutput, calls=%fused_computation.2 | convolution fusion | flops 3233808384 | bytes 45613056 | tf_op jit(solution)/shard_map/lrk,lck->lrc/dot_general | solution.py:10
  260.8 9.6 %copy.13 = bf16[384,8,8,256]{3,2,1,0:T(8,128)(2,1)S(1)} copy(bf16[384,8,8,256]{3,1,2,0:T(8,128)(2,1)} %bitcast.52) | data formatting | bytes 25165824
  270.5 6.2 %copy.10 = bf16[1,6,2,256,8,256]{5,3,0,4,2,1:T(8,128)(2,1)S(1)} copy(bf16[1,6,2,256,8,256]{5,4,3,2,1,0:T(8,128)(2,1)S(1)} %bitcast.55) | data formatting | bytes 25165824 | tf_op jit(solution)/shard_map/stack | solution.py:14
  276.7 9.9 %maximum_bitcast_fusion = bf16[6,2,8,2,256,256]{5,4,3,2,1,0:T(8,128)(2,1)} fusion(bf16[1,6,2,256,8,256]{5,3,0,4,2,1:T(8,128)(2,1)S(1)} %copy.10, bf16[1,6,2,256,8,256]{5,3,0,4,2,1:T(8,128)(2,1)S(1)} %bitcast.57), kind=kLoop, calls=%fused_computation.1 | loop fusion | flops 12582912 | bytes 50331648 | tf_op jit(solution)/shard_map/transpose | solution.py:37
  286.6 25.1 %reshape_reshape.3 = bf16[96,131072]{1,0:T(8,128)(2,1)} reshape(bf16[6,2,8,2,256,256]{5,4,3,2,1,0:T(8,128)(2,1)} %maximum_bitcast_fusion) | data formatting | bytes 50331648 | tf_op jit(solution)/shard_map/reshape;reshape | solution.py:47
  311.8 12.0 %convolution_convert_fusion = bf16[16,131072]{1,0:T(8,128)(2,1)} fusion(bf16[96,131072]{1,0:T(8,128)(2,1)} %reshape_reshape.3, s32[96]{0:T(128)S(1)} %add.18), kind=kOutput, calls=%fused_computation | convolution fusion | flops 404751872 | bytes 29360512 | tf_op jit(solution)/shard_map/dot_general | solution.py:47
  323.8 5.5 %all_to_all.6 = bf16[8,2,131072]{2,1,0:T(2,128)(2,1)} reshape(bf16[16,131072]{1,0:T(8,128)(2,1)} %convolution_convert_fusion) | data formatting | bytes 8388608 | tf_op jit(solution)/shard_map/all_to_all | solution.py:48
  329.3 6.1 %all-to-all-start = ((bf16[8,2,131072]{2,1,0:T(2,128)(2,1)}), bf16[8,2,131072]{2,1,0:T(2,128)(2,1)}, u32[]{:S(2)}, u32[]{:S(2)}) async-start(bf16[8,2,131072]{2,1,0:T(2,128)(2,1)} %all_to_all.6), calls=%async_computation | async-start | bytes 8388608 | tf_op jit(solution)/shard_map/all_to_all | solution.py:48
  335.4 1.9 pad_maximum_fusion
  337.3 90.8 %all-to-all-done = bf16[8,2,131072]{2,1,0:T(2,128)(2,1)} async-done(((bf16[8,2,131072]{2,1,0:T(2,128)(2,1)}), bf16[8,2,131072]{2,1,0:T(2,128)(2,1)}, u32[]{:S(2)}, u32[]{:S(2)}) %all-to-all-start) | async-done | bytes 4194336 | tf_op jit(solution)/shard_map/all_to_all | solution.py:48
  428.1 6.3 %convert_reduce_fusion = f32[2,131072]{1,0:T(2,128)S(1)} fusion(bf16[8,2,131072]{2,1,0:T(2,128)(2,1)} %all-to-all-done), kind=kLoop, calls=%fused_computation.5 | loop fusion | flops 3932160 | bytes 5242880 | tf_op jit(solution)/shard_map/reduce_sum | solution.py:51
  434.4 0.1 copy.14
  434.5 0.1 copy.11
  434.6 1.1 bitcast_subtract_fusion
  (21 shorter events, 0.1 us)
Async XLA Ops:
  7.2 46.3 %all-gather.2.cloned.1.call-start = ((), (), s32[]{:S(2)}) async-start(), calls=%async_computation.1 | async-start | bytes 1966080 | tf_op jit(solution)/shard_map/all_gather | solution.py:18
  7.2 6.2 %collective-permute-start = (bf16[2,6,512,256]{3,2,1,0:T(8,128)(2,1)}, bf16[2,6,512,256]{3,2,1,0:T(8,128)(2,1)}, u32[]{:S(2)}, u32[]{:S(2)}) collective-permute-start(bf16[2,6,512,256]{3,2,1,0:T(8,128)(2,1)} %param.5), channel_id=1, source_target_pairs={{0,8},{8,0},{16,24},{24,16},{1,9},{9,1},{17,25},{25,17},{2,10},{10... | collective-permute-start | bytes 9437192 | tf_op jit(solution)/shard_map/ppermute | solution.py:25
  7.8 17.1 %copy-start.4 = (s32[6,2,8]{2,1,0:T(2,128)S(1)}, s32[6,2,8]{2,1,0:T(2,128)}, u32[]{:S(2)}) copy-start(s32[6,2,8]{2,1,0:T(2,128)} %param.8) | copy-start | bytes 1156
  7.8 17.1 %copy-start.5 = (s32[6,2,8]{2,1,0:T(2,128)S(1)}, s32[6,2,8]{2,1,0:T(2,128)}, u32[]{:S(2)}) copy-start(s32[6,2,8]{2,1,0:T(2,128)} %param.7) | copy-start | bytes 1156
  7.8 45.7 %copy-start = (bf16[2,6,512,256]{3,2,1,0:T(8,128)(2,1)S(1)}, bf16[2,6,512,256]{3,2,1,0:T(8,128)(2,1)}, u32[]{:S(2)}) copy-start(bf16[2,6,512,256]{3,2,1,0:T(8,128)(2,1)} %param.5) | copy-start | bytes 9437188
  22.0 147.4 %collective-permute-start.1 = (bf16[2,6,1024,256]{3,2,1,0:T(8,128)(2,1)}, bf16[2,6,1024,256]{3,2,1,0:T(8,128)(2,1)}, u32[]{:S(2)}, u32[]{:S(2)}) collective-permute-start(bf16[2,6,1024,256]{3,2,1,0:T(8,128)(2,1)} %maximum_select_fusion.1), channel_id=1, source_target_pairs={{0,16},{8,24},{16,0},{24,8},{1,17},{9,25},{17,1},{25,9},{2,18},{10... | collective-permute-start | bytes 18874376 | tf_op jit(solution)/shard_map/ppermute | solution.py:25
  53.5 3.6 copy-start.1
  53.5 3.6 copy-start.2
  260.8 15.8 %slice-start = ((s8[12582912]{0:T(1024)(128)(4,1)}), s8[4194304]{0:T(1024)(128)(4,1)S(1)}, s32[]{:S(2)}) async-start(s8[12582912]{0:T(1024)(128)(4,1)} %bitcast.56), calls=%async_computation.2 | async-start | bytes 8388608
  260.8 15.8 %slice-start.1 = ((s8[12582912]{0:T(1024)(128)(4,1)}), s8[4194304]{0:T(1024)(128)(4,1)S(1)}, s32[]{:S(2)}) async-start(s8[12582912]{0:T(1024)(128)(4,1)} %bitcast.56), calls=%async_computation.3 | async-start | bytes 8388608
  270.5 6.2 %slice-start.2 = ((s8[12582912]{0:T(1024)(128)(4,1)}), s8[4194304]{0:T(1024)(128)(4,1)S(1)}, s32[]{:S(2)}) async-start(s8[12582912]{0:T(1024)(128)(4,1)} %bitcast.56), calls=%async_computation.4 | async-start | bytes 8388608
  329.3 98.8 %all-to-all-start = ((bf16[8,2,131072]{2,1,0:T(2,128)(2,1)}), bf16[8,2,131072]{2,1,0:T(2,128)(2,1)}, u32[]{:S(2)}, u32[]{:S(2)}) async-start(bf16[8,2,131072]{2,1,0:T(2,128)(2,1)} %all_to_all.6), calls=%async_computation | async-start | bytes 8388608 | tf_op jit(solution)/shard_map/all_to_all | solution.py:48
  337.3 97.3 %copy-start.3 = (f32[2,512,256]{2,1,0:T(8,128)S(1)}, f32[2,512,256]{2,1,0:T(8,128)}, u32[]{:S(2)}) copy-start(f32[2,512,256]{2,1,0:T(8,128)} %param.9) | copy-start | bytes 3145732
Sparse Core Ops, SparseCore 0:
  25.0 28.4 all-gather.1
